TPU v7x, 32 devices: a whole 2x2x4 slice. The times are simulated.
32 devices in a mesh: gx: 2 (over x), gy: 4 (over z), gz: 4 (over y, core).
Axes of the slice: x: 2, y: 2, z: 4, core: 2. Of those that a mesh axis runs over, the one named last changes fastest.
Arguments:
- particle_mass: float32 [1048576], P(('gx', 'gy', 'gz')), may hold values from 0.5 to 2
- particle_velocity: float32 [3, 1048576], P(None, ('gx', 'gy', 'gz')), may hold values from -6 to 6
- particle_affine: float32 [9, 1048576], P(None, ('gx', 'gy', 'gz')), may hold values from -6 to 6
- particle_cell: int32 [3, 1048576], P(None, ('gx', 'gy', 'gz')), may hold values from 0 to 13
- particle_fraction: int32 [3, 1048576], P(None, ('gx', 'gy', 'gz')), may hold values from 0 to 1023
- block_owner: int32 [2048, 1], P(('gx', 'gy', 'gz')), may hold values from 0 to 15; in each aligned block of 64 rows (0 to 63, 64 to 127, ...) at most 8 rows name the same one
- block_slot: int32 [2048], P(('gx', 'gy', 'gz')), may hold values from 0 to 31
- block_count: int32 [2048], P(('gx', 'gy', 'gz')), may hold values from 128 to 512
- cell_drag: float32 [1024, 4096], P(('gx', 'gy', 'gz')), may hold values from 0.5 to 2
Outputs:
- grid_velocity: float32 [1024, 3, 4096], P(('gx', 'gy', 'gz'))
- new_velocity: float32 [3, 1048576], P(None, ('gx', 'gy', 'gz'))
- new_affine: float32 [9, 1048576], P(None, ('gx', 'gy', 'gz'))
Inputs may be any that keep to these rules, and one draw needn't show every extreme that they name: `block_owner`: owner index counted over the devices with the particle device's own gx index, in gy+gz order; among the rows of one device, no owner is named more than 8 times. `block_count`: slots at or beyond the count are absent. `particle_cell`: A particle's three stencil nodes lie inside its grid block.
All inputs are finite; a program needn't handle non-finite values.
Results may differ from a plain program's by a relative error of at most 0.0085.
Values may be sent and summed in bfloat16 or wider, within the bound.
A program may use at most 128 MiB of HBM per device.

v0:
```python
import jax
import jax.numpy as jnp
from jax import lax
from jax.sharding import PartitionSpec as P

EDGE = 16
QUANT = 1024
batch_blocks = 4


def spline(offset):
    magnitude = jnp.abs(offset)
    inner_part = 0.75 - magnitude * magnitude
    outer_part = 0.5 * (1.5 - magnitude) * (1.5 - magnitude)
    return jnp.where(magnitude < 0.5, inner_part, jnp.where(magnitude < 1.5, outer_part, 0.0))


def particle_table(
    particle_mass, particle_velocity, particle_affine, particle_cell, particle_fraction, block_count
):
    blocks = block_count.shape[0]
    batch_shape = (blocks, particle_mass.shape[0] // blocks)
    places = jnp.arange(batch_shape[1], dtype=jnp.int32)
    present = places[None, :] < block_count[:, None]
    live_mass = jnp.where(present, particle_mass.reshape(batch_shape), 0.0)
    position = (
        particle_cell.astype(jnp.float32)
        + 0.5
        + (particle_fraction.astype(jnp.float32) + 0.5) / QUANT
    )
    return jnp.concatenate(
        [
            live_mass[None],
            particle_velocity.reshape((3,) + batch_shape),
            particle_affine.reshape((9,) + batch_shape),
            position.reshape((3,) + batch_shape),
        ],
        axis=0,
    )


def stencil(particle_data):
    node_coords = jnp.arange(EDGE, dtype=jnp.float32)
    offset = node_coords[None, :, None, None] - particle_data[13:16][:, None]
    weights = spline(offset)
    return (weights, weights * offset)


def planes(weights, slopes):

    def outer(first_factor, second_factor):
        product_table = first_factor[:, None] * second_factor[None, :]
        return product_table.reshape((EDGE * EDGE,) + product_table.shape[2:]).astype(jnp.bfloat16)

    return (
        outer(weights[1], weights[2]),
        outer(slopes[1], weights[2]),
        outer(weights[1], slopes[2]),
    )


def deposit(particle_data):
    batch_shape = particle_data.shape[1:]
    weights, slopes = stencil(particle_data)
    plane_zero, plane_one, plane_two = planes(weights, slopes)
    live_mass = particle_data[0]
    along_x = weights[0]
    slope_x = slopes[0]
    affine = particle_data[4:13].reshape((3, 3) + batch_shape)
    mass_lead = (live_mass[None] * along_x)[None]
    momentum_lead = live_mass[None, None] * (
        particle_data[1:4][:, None] * along_x[None] + affine[:, 0][:, None] * slope_x[None]
    )
    lead_zero = jnp.concatenate([mass_lead, momentum_lead], axis=0).astype(jnp.bfloat16)
    lead_one = (live_mass[None, None] * affine[:, 1][:, None] * along_x[None]).astype(jnp.bfloat16)
    lead_two = (live_mass[None, None] * affine[:, 2][:, None] * along_x[None]).astype(jnp.bfloat16)

    def contract(lead, plane):
        flattened = lead.reshape((-1,) + batch_shape)
        return jnp.einsum("anp,bnp->nab", flattened, plane, preferred_element_type=jnp.float32)

    count_blocks = batch_shape[0]
    dep_zero = contract(lead_zero, plane_zero).reshape(count_blocks, 4, -1)
    dep_one = contract(lead_one, plane_one).reshape(count_blocks, 3, -1)
    dep_two = contract(lead_two, plane_two).reshape(count_blocks, 3, -1)
    return jnp.concatenate([dep_zero[:, :1], dep_zero[:, 1:] + dep_one + dep_two], axis=1)


def interpolate(particle_data, grid_rows):
    batch_shape = particle_data.shape[1:]
    weights, slopes = stencil(particle_data)
    plane_zero, plane_one, plane_two = planes(weights, slopes)
    along_x = weights[0]
    slope_x = slopes[0]
    flattened = grid_rows.reshape(batch_shape[0], 3 * EDGE, EDGE * EDGE)

    def contract(plane):
        moment = jnp.einsum("nab,bnp->anp", flattened, plane, preferred_element_type=jnp.float32)
        return moment.reshape((3, EDGE) + batch_shape)

    moment_zero = contract(plane_zero)
    moment_one = contract(plane_one)
    moment_two = contract(plane_two)
    velocity_out = jnp.sum(along_x[None] * moment_zero, axis=1)
    column_zero = 4.0 * jnp.sum(slope_x[None] * moment_zero, axis=1)
    column_one = 4.0 * jnp.sum(along_x[None] * moment_one, axis=1)
    column_two = 4.0 * jnp.sum(along_x[None] * moment_two, axis=1)
    affine_out = jnp.stack([column_zero, column_one, column_two], axis=1).reshape(
        (9,) + batch_shape
    )
    present = (particle_data[0] > 0.0).astype(jnp.float32)
    return jnp.concatenate([velocity_out, affine_out], axis=0) * present[None]


def deposit_all(particle_data):
    block_total = particle_data.shape[1]

    def deposit_advance(state_carry, step_index):
        portion = lax.dynamic_slice_in_dim(
            particle_data, step_index * batch_blocks, batch_blocks, 1
        )
        return (state_carry, deposit(portion))

    unused, stacked = lax.scan(
        deposit_advance,
        jnp.zeros((), jnp.float32),
        jnp.arange(block_total // batch_blocks, dtype=jnp.int32),
    )
    return stacked.reshape((block_total,) + stacked.shape[2:])


def interpolate_all(particle_data, grid_rows):
    block_total = particle_data.shape[1]

    def interpolate_advance(step_index, result):
        first_block = step_index * batch_blocks
        portion = lax.dynamic_slice_in_dim(particle_data, first_block, batch_blocks, 1)
        cell_rows = lax.dynamic_slice_in_dim(grid_rows, first_block, batch_blocks, 0)
        return lax.dynamic_update_slice_in_dim(
            result, interpolate(portion, cell_rows), first_block, 1
        )

    initial = jnp.zeros((12, block_total, particle_data.shape[2]), jnp.float32)
    return lax.fori_loop(0, block_total // batch_blocks, interpolate_advance, initial)


def send_slots(owners, group_size, capacity):
    targets = jnp.arange(group_size, dtype=jnp.int32)
    matches = (owners[:, None] == targets[None, :]).astype(jnp.int32)
    earlier = jnp.cumsum(matches, axis=0) - matches
    ranking = jnp.sum(earlier * matches, axis=1)
    return owners * capacity + ranking


def slot_sources(destination, slot_count):
    positions = jnp.arange(slot_count, dtype=jnp.int32)
    matches = destination[None, :] == positions[:, None]
    block_numbers = jnp.arange(destination.shape[0], dtype=jnp.int32)
    source = jnp.sum(jnp.where(matches, block_numbers[None, :], 0), axis=1)
    return (source, jnp.any(matches, axis=1))


def match_tiles(arrived_tiles, tile_count):
    tile_numbers = jnp.arange(tile_count, dtype=jnp.float32)
    return (arrived_tiles[None, :] == tile_numbers[:, None]).astype(jnp.float32)


def update_grid(deposits, tile_match, cell_drag):
    tile_count = tile_match.shape[0]
    flattened = deposits.reshape(deposits.shape[0], -1)
    summed = jnp.dot(
        tile_match, flattened, precision=lax.Precision.HIGHEST, preferred_element_type=jnp.float32
    )
    summed = summed.reshape((tile_count,) + deposits.shape[1:])
    grid_velocity = summed[:, 1:] / (summed[:, :1] + cell_drag[:, None, :])
    rounded = grid_velocity.astype(jnp.bfloat16)
    picked = jnp.dot(
        tile_match.T.astype(jnp.bfloat16),
        rounded.reshape(tile_count, -1),
        preferred_element_type=jnp.float32,
    )
    cell_rows = picked.astype(jnp.bfloat16).reshape((deposits.shape[0], 3, -1))
    return (grid_velocity, cell_rows)


def per_device(
    particle_mass,
    particle_velocity,
    particle_affine,
    particle_cell,
    particle_fraction,
    block_owner,
    block_slot,
    block_count,
    cell_drag,
):
    group_size = lax.axis_size(("gy", "gz"))
    blocks = block_count.shape[0]
    capacity = max(1, 2 * blocks // group_size)
    slot_count = group_size * capacity
    tile_count = cell_drag.shape[0]
    particle_data = particle_table(
        particle_mass,
        particle_velocity,
        particle_affine,
        particle_cell,
        particle_fraction,
        block_count,
    )
    destination = send_slots(block_owner[:, 0], group_size, capacity)
    source, filled = slot_sources(destination, slot_count)
    tile_ids = jnp.where(filled, jnp.take(block_slot, source), -1).astype(jnp.float32)
    deposits = deposit_all(particle_data)
    outgoing = jnp.where(filled[:, None, None], jnp.take(deposits, source, axis=0), 0.0)
    arrived, arrived_tiles = (
        lax.all_to_all(outgoing, ("gy", "gz"), split_axis=0, concat_axis=0, tiled=True),
        lax.all_to_all(tile_ids, ("gy", "gz"), split_axis=0, concat_axis=0, tiled=True),
    )
    tile_match = match_tiles(arrived_tiles, tile_count)
    grid_velocity, cell_rows = update_grid(arrived, tile_match, cell_drag)
    returned = lax.all_to_all(cell_rows, ("gy", "gz"), split_axis=0, concat_axis=0, tiled=True)
    finished = interpolate_all(particle_data, jnp.take(returned, destination, axis=0))
    new_velocity = finished[:3].reshape(3, -1)
    new_affine = finished[3:].reshape(9, -1)
    return (grid_velocity, new_velocity, new_affine)


def solution(mesh):
    return jax.shard_map(
        per_device,
        mesh=mesh,
        in_specs=(
            P(("gx", "gy", "gz")),
            P(None, ("gx", "gy", "gz")),
            P(None, ("gx", "gy", "gz")),
            P(None, ("gx", "gy", "gz")),
            P(None, ("gx", "gy", "gz")),
            P(("gx", "gy", "gz"), None),
            P(("gx", "gy", "gz")),
            P(("gx", "gy", "gz")),
            P(("gx", "gy", "gz"), None),
        ),
        out_specs=(
            P(("gx", "gy", "gz"), None, None),
            P(None, ("gx", "gy", "gz")),
            P(None, ("gx", "gy", "gz")),
        ),
        check_vma=False,
    )
```

profile of v0, /device:TPU:13, one launch (start us, length us, event | category | flops | bytes accessed | tf_op | source)
XLA Modules:
  0.0 659.1 jit_solution(10529736568579550010)
XLA Ops:
  5.6 6.5 all-to-all-start
  12.2 2.8 copy.92
  18.4 167.9 %while.23 = (s32[]{:T(128)}, f32[16,4,4,4096]{3,2,1,0:T(4,128)}, s32[16]{0:T(128)S(1)}, f32[16,64,512]{2,1,0:T(8,128)}, s32[]{:T(128)}, /*index=5*/s32[]{:T(128)...) while((s32[]{:T(128)}, f32[16,4,4,4096]{3,2,1,0:T(4,128)}, s32[16]{0:T(128)S(1)}, ...), condition=%wide.region_5.6_spmd, body=%wide.region_4.5_spmd.sunk | while | flops 173355008 | bytes 15483619 | solution.py:124
  186.2 11.4 %gather_fusion.1 = f32[128,4,4096]{2,1,0:T(4,128)} fusion(f32[64,4,4096]{2,1,0:T(4,128)} %bitcast.211, s32[1024]{0:T(1024)S(1)} %pad_clamp_fusion.1), kind=kCustom, calls=%fused_computation.1 | custom fusion | bytes 16777728 | tf_op jit(solution)/shard_map/jit(_take)/gather | solution.py:214
  197.7 11.6 %select_select_fusion = f32[128,4,4096]{2,1,0:T(4,128)} fusion(f32[128,4,4096]{2,1,0:T(4,128)} %gather_fusion.1, pred[128]{0:T(512)(128)(4,1)S(1)} %compare_and_fusion, pred[128]{0:T(512)(128)(4,1)S(1)} %fusion.22), kind=kLoop, calls=%fused_computation.72 | loop fusion | flops 4194304 | bytes 16777472 | tf_op jit(solution)/shard_map/jit(_where)/select_n | solution.py:214
  209.3 6.0 all-to-all-start.1
  216.6 181.1 %all-to-all-done.1 = f32[128,4,4096]{2,1,0:T(4,128)} async-done(((f32[128,4,4096]{2,1,0:T(4,128)}), f32[128,4,4096]{2,1,0:T(4,128)}, u32[]{:S(2)}, u32[]{:S(2)}) %all-to-all-start.1) | async-done | bytes 8388640 | tf_op jit(solution)/shard_map/all_to_all | solution.py:216
  397.7 10.0 %copy.86 = f32[128,4,4096]{0,2,1:T(8,128)} copy(f32[128,4,4096]{2,1,0:T(4,128)} %all-to-all-done.1) | data formatting | bytes 16777216 | tf_op jit(solution)/shard_map/all_to_all | solution.py:216
  407.7 8.1 %fusion.17 = f32[32,4,4096]{2,0,1:T(8,128)S(1)} fusion(f32[128,4,4096]{0,2,1:T(8,128)} %copy.86, f32[128]{0:T(128)S(1)} %eq.54), kind=kOutput, calls=%fused_computation.70 | convolution fusion | flops 805310464 | bytes 10486272 | tf_op jit(solution)/shard_map/dot_general | solution.py:171
  417.3 2.7 convolution_convert_fusion
  420.0 3.5 copy.88
  423.5 5.5 copy.89
  429.0 4.9 all-to-all-start.2
  433.9 92.4 %all-to-all-done.2 = bf16[128,3,4096]{2,1,0:T(4,128)(2,1)} async-done(((bf16[128,3,4096]{2,1,0:T(4,128)(2,1)}), bf16[128,3,4096]{2,1,0:T(4,128)(2,1)}, u32[]{:S(2)}, u32[]{:S(2)}) %all-to-all-start.2) | async-done | bytes 3145760 | tf_op jit(solution)/shard_map/all_to_all | solution.py:221
  526.3 4.5 gather_fusion.2
  530.9 2.4 broadcast_select_fusion
  534.6 118.2 %while.24 = (s32[]{:T(128)}, f32[12,64,512]{2,1,0:T(8,128)}, f32[16,64,512]{2,1,0:T(8,128)}, bf16[64,3,4096]{2,1,0:T(4,128)(2,1)}, s32[]{:T(128)}, /*index=5*/s32[]{:T(128)}, s32[]{:T(128)}, s32[]{:T(128)}, s32[]{}) while((s32[]{:T(128)}, f32[12,64,512]{2,1,0:T(8,128)}, f32[16,64,512]{2,1,0:T(8,128)}, bf16[64,3,4096]{2,1,0:T(4,128)(2,1)}, ...), condition=%wide.region_11.12_spmd, body=%wide.region_6.11_spmd.sunk | while | flops 156190720 | bytes 13369515 | solution.py:144
  536.6 1.6 constant_dynamic-slice_fusion.11
  544.0 1.6 constant_dynamic-slice_fusion.11
  551.3 1.6 constant_dynamic-slice_fusion.11
  558.7 1.6 constant_dynamic-slice_fusion.11
  566.1 1.6 constant_dynamic-slice_fusion.11
  573.5 1.6 constant_dynamic-slice_fusion.11
  580.9 1.6 constant_dynamic-slice_fusion.11
  588.2 1.6 constant_dynamic-slice_fusion.11
  595.6 1.6 constant_dynamic-slice_fusion.11
  603.0 1.6 constant_dynamic-slice_fusion.11
  617.8 1.6 constant_dynamic-slice_fusion.11
  625.2 1.6 constant_dynamic-slice_fusion.11
  632.6 1.6 constant_dynamic-slice_fusion.11
  647.4 1.6 constant_dynamic-slice_fusion.11
  655.5 2.5 copy.95
  (732 shorter events, 265.7 us)
Async XLA Ops:
  0.6 2.7 copy-start
  5.6 203.7 %all-to-all-start = ((f32[16,8,1]{1,2,0:T(1,128)}), f32[16,8,1]{1,2,0:T(1,128)S(1)}, u32[]{:S(2)}, u32[]{:S(2)}) async-start(f32[16,8,1]{1,2,0:T(1,128)} %copy.85), calls=%async_computation | async-start | bytes 16384 | tf_op jit(solution)/shard_map/all_to_all | solution.py:217
  15.0 0.9 copy-start.6
  15.0 1.1 copy-start.2
  15.0 1.3 copy-start.3
  15.0 1.5 copy-start.4
  15.9 0.8 copy-start.8
  209.3 188.4 %all-to-all-start.1 = ((f32[128,4,4096]{2,1,0:T(4,128)}), f32[128,4,4096]{2,1,0:T(4,128)}, u32[]{:S(2)}, u32[]{:S(2)}) async-start(f32[128,4,4096]{2,1,0:T(4,128)} %select_select_fusion), calls=%async_computation.1 | async-start | bytes 16777216 | tf_op jit(solution)/shard_map/all_to_all | solution.py:216
  407.7 8.1 %copy-start.5 = (f32[32,4096]{1,0:T(8,128)S(1)}, f32[32,4096]{1,0:T(8,128)}, u32[]{:S(2)}) copy-start(f32[32,4096]{1,0:T(8,128)} %param.21) | copy-start | bytes 1572868
  429.0 4.9 copy-start.7
  429.0 97.4 %all-to-all-start.2 = ((bf16[128,3,4096]{2,1,0:T(4,128)(2,1)}), bf16[128,3,4096]{2,1,0:T(4,128)(2,1)}, u32[]{:S(2)}, u32[]{:S(2)}) async-start(bf16[128,3,4096]{2,1,0:T(4,128)(2,1)} %copy.89), calls=%async_computation.2 | async-start | bytes 8388608 | tf_op jit(solution)/shard_map/all_to_all | solution.py:221
  655.5 3.6 copy-start.1
where the time goes:
time: 665 us; the launch traced here: 659 us
  waiting for transfers between devices  274 us (41%)
  local copies, waits for them, and re-layouts  164 us (25%)
  other arithmetic  114 us (17%)
  matrix products  74.8 us (11%)
  starting transfers between devices  17.4 us (3%)
  loops' own time  13.9 us (2%)
    all_to_all x1, waiting for transfers between devices, per_device(): lax.all_to_all(outgoing, ('gy', 'gz'), split_axis=0, concat_axis=0, tiled...  181 us
    all_to_all x1, waiting for transfers between devices, per_device(): lax.all_to_all(cell_rows, ('gy', 'gz'), split_axis=0, concat_axis=0, tile...  92.4 us
    dot_general x48, matrix products, contract(): jnp.einsum('anp,bnp->nab', flattened, plane, preferred_element_type=jnp.f...  50.1 us
    convert_element_type x32, other arithmetic, outer(): product_table.reshape((EDGE * EDGE,) + product_table.shape[2:])  29 us
    dynamic_slice x16, local copies, waits for them, and re-layouts, interpolate_advance(): lax.dynamic_slice_in_dim(grid_rows, first_block, batch_blocks, 0)  25.8 us
    reshape x16, local copies, waits for them, and re-layouts, interpolate(): flattened = grid_rows.reshape(batch_shape[0], 3 * EDGE, EDGE * EDGE)  16.8 us
    slice x16, local copies, waits for them, and re-layouts, deposit(): affine = particle_data[4:13].reshape((3, 3) + batch_shape)  14.9 us
    another operation x32, other arithmetic  14.9 us
  transfers between devices with their start and end apart: 3, of which 2 were waited for; matrix products, arithmetic and copies ran while one was open for 28% of the time, Pallas kernels for 0%

commit v1 on v0

--- a/solution.py
+++ b/solution.py
@@ -218,7 +218,19 @@
     )
     tile_match = match_tiles(arrived_tiles, tile_count)
     grid_velocity, cell_rows = update_grid(arrived, tile_match, cell_drag)
-    returned = lax.all_to_all(cell_rows, ("gy", "gz"), split_axis=0, concat_axis=0, tiled=True)
+    ways, here = (lax.axis_size(("gy", "gz")), lax.axis_index(("gy", "gz")))
+    width = cell_rows.shape[0] // ways
+    dims = list(cell_rows.shape)
+    dims[0] = width
+    height = dims[0]
+    dims[0] = height * ways
+    full = jnp.zeros(dims, cell_rows.dtype)
+    for mask in range(ways):
+        part = lax.dynamic_slice_in_dim(cell_rows, (here ^ mask) * width, width, axis=0)
+        if mask:
+            part = lax.ppermute(part, ("gy", "gz"), [(d, d ^ mask) for d in range(ways)])
+        full = lax.dynamic_update_slice_in_dim(full, part, (here ^ mask) * height, axis=0)
+    returned = full
     finished = interpolate_all(particle_data, jnp.take(returned, destination, axis=0))
     new_velocity = finished[:3].reshape(3, -1)
     new_affine = finished[3:].reshape(9, -1)

time: 665 us -> 767 us (1.15); the launches traced: 659 us -> 752 us
  local copies, waits for them, and re-layouts: 164 us -> 268 us
  waiting for transfers between devices: 274 us -> 253 us
  starting transfers between devices: 17.4 us -> 26.4 us
    all_to_all x1 -> x0, waiting for transfers between devices: 92.4 us -> none  [per_device(): lax.all_to_all(cell_rows, ('gy', 'gz'), split_axis=0, concat_axis=0, tile...]
    ppermute x0 -> x15, waiting for transfers between devices: none -> 72.4 us  [per_device(): lax.ppermute(part, ('gy', 'gz'), [(d, d ^ mask) for d in range(ways)])]
    unnamed x23 -> x57, local copies, waits for them, and re-layouts: 8.83 us -> 63.9 us
    dynamic_slice x0 -> x1, local copies, waits for them, and re-layouts: none -> 20.2 us  [per_device(): lax.dynamic_slice_in_dim(cell_rows, (here ^ mask) * width, width, axis=0)]
    dynamic_update_slice x0 -> x16, local copies, waits for them, and re-layouts: none -> 17.6 us  [per_device(): lax.dynamic_update_slice_in_dim(full, part, (here ^ mask) * height, axis=0)]
    ppermute x0 -> x15, starting transfers between devices: none -> 13.8 us  [per_device(): lax.ppermute(part, ('gy', 'gz'), [(d, d ^ mask) for d in range(ways)])]
    gather x1, local copies, waits for them, and re-layouts: 11.4 us -> 23.3 us  [per_device(): jnp.take(deposits, source, axis=0)]
  transfers between devices with their start and end apart: 3 -> 17, of which waited for: 2 -> 9; matrix products, arithmetic and copies ran while one was open for 28% -> 35% of each run, Pallas kernels for 0% -> 0%
where the time goes in v1:
time: 767 us; the launch traced here: 752 us
  local copies, waits for them, and re-layouts  268 us (35%)
  waiting for transfers between devices  253 us (33%)
  other arithmetic  114 us (15%)
  matrix products  74.8 us (10%)
  starting transfers between devices  26.4 us (3%)
  loops' own time  14.2 us (2%)
    all_to_all x1, waiting for transfers between devices, per_device(): lax.all_to_all(outgoing, ('gy', 'gz'), split_axis=0, concat_axis=0, tiled...  181 us
    ppermute x15, waiting for transfers between devices, per_device(): lax.ppermute(part, ('gy', 'gz'), [(d, d ^ mask) for d in range(ways)])  72.4 us
    unnamed x57, local copies, waits for them, and re-layouts  63.9 us
    dot_general x48, matrix products, contract(): jnp.einsum('anp,bnp->nab', flattened, plane, preferred_element_type=jnp.f...  50.1 us
    convert_element_type x32, other arithmetic, outer(): product_table.reshape((EDGE * EDGE,) + product_table.shape[2:])  29 us
    dynamic_slice x16, local copies, waits for them, and re-layouts, interpolate_advance(): lax.dynamic_slice_in_dim(grid_rows, first_block, batch_blocks, 0)  25.8 us
    gather x1, local copies, waits for them, and re-layouts, per_device(): jnp.take(deposits, source, axis=0)  23.3 us
    dynamic_slice x1, local copies, waits for them, and re-layouts, per_device(): lax.dynamic_slice_in_dim(cell_rows, (here ^ mask) * width, width, axis=0)  20.2 us
  transfers between devices with their start and end apart: 17, of which 9 were waited for; matrix products, arithmetic and copies ran while one was open for 35% of the time, Pallas kernels for 0%

profile of v1, /device:TPU:13, one launch (start us, length us, event | category | flops | bytes accessed | tf_op | source)
XLA Modules:
  0.0 752.3 jit_solution(17068218777026984747)
XLA Ops:
  5.6 6.5 all-to-all-start
  12.2 2.9 copy.182
  18.1 167.9 %while.23 = (s32[]{:T(128)}, f32[16,4,4,4096]{3,2,1,0:T(4,128)}, s32[16]{0:T(128)S(1)}, f32[16,64,512]{2,1,0:T(8,128)}, s32[]{:T(128)}, /*index=5*/s32[]{:T(128)...) while((s32[]{:T(128)}, f32[16,4,4,4096]{3,2,1,0:T(4,128)}, s32[16]{0:T(128)S(1)}, ...), condition=%wide.region_5.6_spmd, body=%wide.region_4.5_spmd.sunk | while | flops 173355008 | bytes 15483619 | solution.py:124
  185.9 23.3 %gather_fusion.1 = f32[128,4,4096]{2,1,0:T(4,128)} fusion(f32[64,4,4096]{2,1,0:T(4,128)} %bitcast.212, s32[1024]{0:T(1024)S(1)} %pad_clamp_fusion.1), kind=kCustom, calls=%fused_computation.1 | custom fusion | bytes 16777728 | tf_op jit(solution)/shard_map/jit(_take)/gather | solution.py:214
  209.2 11.6 %select_select_fusion = f32[128,4,4096]{2,1,0:T(4,128)} fusion(f32[128,4,4096]{2,1,0:T(4,128)} %gather_fusion.1, pred[128]{0:T(512)(128)(4,1)S(1)} %compare_and_fusion, pred[128]{0:T(512)(128)(4,1)S(1)} %fusion.22), kind=kLoop, calls=%fused_computation.72 | loop fusion | flops 4194304 | bytes 16777472 | tf_op jit(solution)/shard_map/jit(_where)/select_n | solution.py:214
  220.9 6.1 all-to-all-start.1
  228.3 181.0 %all-to-all-done.1 = f32[128,4,4096]{2,1,0:T(4,128)} async-done(((f32[128,4,4096]{2,1,0:T(4,128)}), f32[128,4,4096]{2,1,0:T(4,128)}, u32[]{:S(2)}, u32[]{:S(2)}) %all-to-all-start.1) | async-done | bytes 8388640 | tf_op jit(solution)/shard_map/all_to_all | solution.py:216
  409.4 10.0 %copy.145 = f32[128,4,4096]{0,2,1:T(8,128)} copy(f32[128,4,4096]{2,1,0:T(4,128)} %all-to-all-done.1) | data formatting | bytes 16777216 | tf_op jit(solution)/shard_map/all_to_all | solution.py:216
  419.4 8.1 %fusion.17 = f32[32,4,4096]{2,0,1:T(8,128)S(1)} fusion(f32[128,4,4096]{0,2,1:T(8,128)} %copy.145, f32[128]{0:T(128)S(1)} %eq.54), kind=kOutput, calls=%fused_computation.70 | convolution fusion | flops 805310464 | bytes 10486272 | tf_op jit(solution)/shard_map/dot_general | solution.py:171
  431.7 3.5 copy.147
  435.2 20.2 %constant_dynamic-slice_fusion.5 = (bf16[8,3,4096]{0,2,1:T(8,128)(2,1)}, bf16[8,3,4096]{0,2,1:T(8,128)(2,1)}, bf16[8,3,4096]{0,2,1:T(8,128)(2,1)}, bf16[8,3,4096...) fusion(bf16[128,3,4096]{0,2,1:T(8,128)(2,1)S(1)} %bitcast.199, ...), kind=kLoop, calls=%fused_computation.98 | loop fusion | bytes 6291520 | tf_op jit(solution)/shard_map/dynamic_slice | solution.py:229
  455.4 3.5 copy.164
  458.9 4.0 copy.165
  465.6 4.1 copy.167
  471.8 3.9 copy.168
  479.9 4.0 broadcast_in_dim.121
  487.4 4.1 copy.171
  491.5 4.0 copy.172
  498.1 4.1 copy.174
  502.2 4.0 copy.175
  508.8 4.1 copy.177
  513.0 4.0 copy.178
  538.8 22.0 %collective-permute-done.7 = bf16[8,3,4096]{2,1,0:T(4,128)(2,1)S(1)} collective-permute-done((bf16[8,3,4096]{2,1,0:T(4,128)(2,1)}, bf16[8,3,4096]{2,1,0:T(4,128)(2,1)S(1)}, u32[]{:S(2)}, u32[]{:S(2)}) %collective-permute-start.7) | collective-permute-done | bytes 196640 | tf_op jit(solution)/shard_map/ppermute | solution.py:231
  561.6 10.4 %collective-permute-done.8 = bf16[8,3,4096]{2,1,0:T(4,128)(2,1)S(1)} collective-permute-done((bf16[8,3,4096]{2,1,0:T(4,128)(2,1)}, bf16[8,3,4096]{2,1,0:T(4,128)(2,1)S(1)}, u32[]{:S(2)}, u32[]{:S(2)}) %collective-permute-start.8) | collective-permute-done | bytes 196640 | tf_op jit(solution)/shard_map/ppermute | solution.py:231
  572.9 10.6 %collective-permute-done.9 = bf16[8,3,4096]{2,1,0:T(4,128)(2,1)S(1)} collective-permute-done((bf16[8,3,4096]{2,1,0:T(4,128)(2,1)}, bf16[8,3,4096]{2,1,0:T(4,128)(2,1)S(1)}, u32[]{:S(2)}, u32[]{:S(2)}) %collective-permute-start.9) | collective-permute-done | bytes 196640 | tf_op jit(solution)/shard_map/ppermute | solution.py:231
  585.3 3.7 collective-permute-done.10
  589.9 11.5 %collective-permute-done.11 = bf16[8,3,4096]{2,1,0:T(4,128)(2,1)S(1)} collective-permute-done((bf16[8,3,4096]{2,1,0:T(4,128)(2,1)S(1)}, bf16[8,3,4096]{2,1,0:T(4,128)(2,1)S(1)}, u32[]{:S(2)}, u32[]{:S(2)}) %collective-permute-start.11) | collective-permute-done | bytes 196640 | tf_op jit(solution)/shard_map/ppermute | solution.py:231
  602.2 4.8 collective-permute-done.12
  607.8 4.3 collective-permute-done.13
  612.9 5.0 collective-permute-done.14
  618.7 4.5 gather_fusion.2
  627.0 118.6 %while.24 = (s32[]{:T(128)}, f32[12,64,512]{2,1,0:T(8,128)}, f32[16,64,512]{2,1,0:T(8,128)}, bf16[64,3,4096]{2,1,0:T(4,128)(2,1)}, s32[]{:T(128)}, /*index=5*/s32[]{:T(128)}, s32[]{:T(128)}, s32[]{:T(128)}, s32[]{}) while((s32[]{:T(128)}, f32[12,64,512]{2,1,0:T(8,128)}, f32[16,64,512]{2,1,0:T(8,128)}, bf16[64,3,4096]{2,1,0:T(4,128)(2,1)}, ...), condition=%wide.region_11.12_spmd, body=%wide.region_6.11_spmd.sunk | while | flops 156190720 | bytes 13369515 | solution.py:144
  (811 shorter events, 342.6 us)
Async XLA Ops:
  5.6 215.2 %all-to-all-start = ((f32[16,8,1]{1,2,0:T(1,128)}), f32[16,8,1]{1,2,0:T(1,128)S(1)}, u32[]{:S(2)}, u32[]{:S(2)}) async-start(f32[16,8,1]{1,2,0:T(1,128)} %copy.144), calls=%async_computation | async-start | bytes 16384 | tf_op jit(solution)/shard_map/all_to_all | solution.py:217
  12.2 3.1 copy-start.15
  12.2 3.1 copy-start.8
  12.2 3.1 copy-start.9
  220.9 6.2 copy-start.16
  220.9 188.5 %all-to-all-start.1 = ((f32[128,4,4096]{2,1,0:T(4,128)}), f32[128,4,4096]{2,1,0:T(4,128)}, u32[]{:S(2)}, u32[]{:S(2)}) async-start(f32[128,4,4096]{2,1,0:T(4,128)} %select_select_fusion), calls=%async_computation.1 | async-start | bytes 16777216 | tf_op jit(solution)/shard_map/all_to_all | solution.py:216
  419.4 8.1 %copy-start.11 = (f32[32,4096]{1,0:T(8,128)S(1)}, f32[32,4096]{1,0:T(8,128)}, u32[]{:S(2)}) copy-start(f32[32,4096]{1,0:T(8,128)} %param.21) | copy-start | bytes 1572868
  455.4 7.6 %copy-start.7 = (bf16[8,3,4096]{0,2,1:T(8,128)(2,1)S(1)}, bf16[8,3,4096]{0,2,1:T(8,128)(2,1)}, u32[]{:S(2)}) copy-start(bf16[8,3,4096]{0,2,1:T(8,128)(2,1)} %get-tuple-element.181) | copy-start | bytes 589828
  462.9 56.2 %collective-permute-start = (bf16[8,3,4096]{2,1,0:T(4,128)(2,1)}, bf16[8,3,4096]{2,1,0:T(4,128)(2,1)}, u32[]{:S(2)}, u32[]{:S(2)}) collective-permute-start(bf16[8,3,4096]{2,1,0:T(4,128)(2,1)} %copy.165), channel_id=1, source_target_pairs={{0,1},{1,0},{2,3},{3,2},{4,5},{5,4},{6,7},{7,6},{8,9},{9,8},{10,11... | collective-permute-start | bytes 589832 | tf_op jit(solution)/shard_map/ppermute | solution.py:231
  465.6 55.4 %collective-permute-start.1 = (bf16[8,3,4096]{2,1,0:T(4,128)(2,1)}, bf16[8,3,4096]{2,1,0:T(4,128)(2,1)}, u32[]{:S(2)}, u32[]{:S(2)}) collective-permute-start(bf16[8,3,4096]{2,1,0:T(4,128)(2,1)} %copy.166), channel_id=1, source_target_pairs={{0,2},{1,3},{2,0},{3,1},{4,6},{5,7},{6,4},{7,5},{8,10},{9,11},{10,... | collective-permute-start | bytes 589832 | tf_op jit(solution)/shard_map/ppermute | solution.py:231
  465.6 10.1 %copy-start.6 = (bf16[8,3,4096]{0,2,1:T(8,128)(2,1)S(1)}, bf16[8,3,4096]{0,2,1:T(8,128)(2,1)}, u32[]{:S(2)}) copy-start(bf16[8,3,4096]{0,2,1:T(8,128)(2,1)} %get-tuple-element.178) | copy-start | bytes 589828
  469.8 55.8 %collective-permute-start.2 = (bf16[8,3,4096]{2,1,0:T(4,128)(2,1)}, bf16[8,3,4096]{2,1,0:T(4,128)(2,1)}, u32[]{:S(2)}, u32[]{:S(2)}) collective-permute-start(bf16[8,3,4096]{2,1,0:T(4,128)(2,1)} %copy.167), channel_id=1, source_target_pairs={{0,3},{1,2},{2,1},{3,0},{4,7},{5,6},{6,5},{7,4},{8,11},{9,10},{10,... | collective-permute-start | bytes 589832 | tf_op jit(solution)/shard_map/ppermute | solution.py:231
  475.7 52.7 %collective-permute-start.3 = (bf16[8,3,4096]{2,1,0:T(4,128)(2,1)}, bf16[8,3,4096]{2,1,0:T(4,128)(2,1)}, u32[]{:S(2)}, u32[]{:S(2)}) collective-permute-start(bf16[8,3,4096]{2,1,0:T(4,128)(2,1)} %copy.168), channel_id=1, source_target_pairs={{0,4},{1,5},{2,6},{3,7},{4,0},{5,1},{6,2},{7,3},{8,12},{9,13},{10,... | collective-permute-start | bytes 589832 | tf_op jit(solution)/shard_map/ppermute | solution.py:231
  478.6 6.1 copy-start.5
  478.6 52.8 %collective-permute-start.4 = (bf16[8,3,4096]{2,1,0:T(4,128)(2,1)}, bf16[8,3,4096]{2,1,0:T(4,128)(2,1)}, u32[]{:S(2)}, u32[]{:S(2)}) collective-permute-start(bf16[8,3,4096]{2,1,0:T(4,128)(2,1)} %copy.169), channel_id=1, source_target_pairs={{0,5},{1,4},{2,7},{3,6},{4,1},{5,0},{6,3},{7,2},{8,13},{9,12},{10,... | collective-permute-start | bytes 589832 | tf_op jit(solution)/shard_map/ppermute | solution.py:231
  487.4 8.1 %copy-start.4 = (bf16[8,3,4096]{0,2,1:T(8,128)(2,1)S(1)}, bf16[8,3,4096]{0,2,1:T(8,128)(2,1)}, u32[]{:S(2)}) copy-start(bf16[8,3,4096]{0,2,1:T(8,128)(2,1)} %get-tuple-element.174) | copy-start | bytes 589828
  498.1 8.1 %copy-start.3 = (bf16[8,3,4096]{0,2,1:T(8,128)(2,1)S(1)}, bf16[8,3,4096]{0,2,1:T(8,128)(2,1)}, u32[]{:S(2)}) copy-start(bf16[8,3,4096]{0,2,1:T(8,128)(2,1)} %get-tuple-element.171) | copy-start | bytes 589828
  508.8 8.1 %copy-start.2 = (bf16[8,3,4096]{0,2,1:T(8,128)(2,1)S(1)}, bf16[8,3,4096]{0,2,1:T(8,128)(2,1)}, u32[]{:S(2)}) copy-start(bf16[8,3,4096]{0,2,1:T(8,128)(2,1)} %get-tuple-element.168) | copy-start | bytes 589828
  519.0 18.8 %copy-start.14 = (bf16[8,3,4096]{2,1,0:T(4,128)(2,1)S(1)}, bf16[8,3,4096]{2,1,0:T(4,128)(2,1)}, u32[]{:S(2)}) copy-start(bf16[8,3,4096]{2,1,0:T(4,128)(2,1)} %copy.176) | copy-start | bytes 589828
  519.0 41.8 %copy-start.13 = (bf16[8,3,4096]{2,1,0:T(4,128)(2,1)S(1)}, bf16[8,3,4096]{2,1,0:T(4,128)(2,1)}, u32[]{:S(2)}) copy-start(bf16[8,3,4096]{2,1,0:T(4,128)(2,1)} %copy.177) | copy-start | bytes 589828
  519.1 53.0 %copy-start.12 = (bf16[8,3,4096]{2,1,0:T(4,128)(2,1)S(1)}, bf16[8,3,4096]{2,1,0:T(4,128)(2,1)}, u32[]{:S(2)}) copy-start(bf16[8,3,4096]{2,1,0:T(4,128)(2,1)} %copy.178) | copy-start | bytes 589828
  519.1 15.4 %collective-permute-start.5 = (bf16[8,3,4096]{2,1,0:T(4,128)(2,1)}, bf16[8,3,4096]{2,1,0:T(4,128)(2,1)S(1)}, u32[]{:S(2)}, u32[]{:S(2)}) collective-permute-start(bf16[8,3,4096]{2,1,0:T(4,128)(2,1)} %copy.170), channel_id=1, source_target_pairs={{0,6},{1,7},{2,4},{3,5},{4,2},{5,3},{6,0},{7,1},{8,14},{9,15},{10,... | collective-permute-start | bytes 589832 | tf_op jit(solution)/shard_map/ppermute | solution.py:231
  521.0 16.9 %collective-permute-start.6 = (bf16[8,3,4096]{2,1,0:T(4,128)(2,1)}, bf16[8,3,4096]{2,1,0:T(4,128)(2,1)S(1)}, u32[]{:S(2)}, u32[]{:S(2)}) collective-permute-start(bf16[8,3,4096]{2,1,0:T(4,128)(2,1)} %copy.171), channel_id=1, source_target_pairs={{0,7},{1,6},{2,5},{3,4},{4,3},{5,2},{6,1},{7,0},{8,15},{9,14},{10,... | collective-permute-start | bytes 589832 | tf_op jit(solution)/shard_map/ppermute | solution.py:231
  525.6 35.2 %collective-permute-start.7 = (bf16[8,3,4096]{2,1,0:T(4,128)(2,1)}, bf16[8,3,4096]{2,1,0:T(4,128)(2,1)S(1)}, u32[]{:S(2)}, u32[]{:S(2)}) collective-permute-start(bf16[8,3,4096]{2,1,0:T(4,128)(2,1)} %copy.172), channel_id=1, source_target_pairs={{0,8},{1,9},{2,10},{3,11},{4,12},{5,13},{6,14},{7,15},{8,0},{9,1},... | collective-permute-start | bytes 589832 | tf_op jit(solution)/shard_map/ppermute | solution.py:231
  528.4 43.6 %collective-permute-start.8 = (bf16[8,3,4096]{2,1,0:T(4,128)(2,1)}, bf16[8,3,4096]{2,1,0:T(4,128)(2,1)S(1)}, u32[]{:S(2)}, u32[]{:S(2)}) collective-permute-start(bf16[8,3,4096]{2,1,0:T(4,128)(2,1)} %copy.173), channel_id=1, source_target_pairs={{0,9},{1,8},{2,11},{3,10},{4,13},{5,12},{6,15},{7,14},{8,1},{9,0},... | collective-permute-start | bytes 589832 | tf_op jit(solution)/shard_map/ppermute | solution.py:231
  531.4 52.0 %collective-permute-start.9 = (bf16[8,3,4096]{2,1,0:T(4,128)(2,1)}, bf16[8,3,4096]{2,1,0:T(4,128)(2,1)S(1)}, u32[]{:S(2)}, u32[]{:S(2)}) collective-permute-start(bf16[8,3,4096]{2,1,0:T(4,128)(2,1)} %copy.174), channel_id=1, source_target_pairs={{0,10},{1,11},{2,8},{3,9},{4,14},{5,15},{6,12},{7,13},{8,2},{9,3},... | collective-permute-start | bytes 589832 | tf_op jit(solution)/shard_map/ppermute | solution.py:231
  534.5 54.6 %collective-permute-start.10 = (bf16[8,3,4096]{2,1,0:T(4,128)(2,1)}, bf16[8,3,4096]{2,1,0:T(4,128)(2,1)S(1)}, u32[]{:S(2)}, u32[]{:S(2)}) collective-permute-start(bf16[8,3,4096]{2,1,0:T(4,128)(2,1)} %copy.175), channel_id=1, source_target_pairs={{0,11},{1,10},{2,9},{3,8},{4,15},{5,14},{6,13},{7,12},{8,3},{9,2},... | collective-permute-start | bytes 589832 | tf_op jit(solution)/shard_map/ppermute | solution.py:231
  537.9 63.5 %collective-permute-start.11 = (bf16[8,3,4096]{2,1,0:T(4,128)(2,1)S(1)}, bf16[8,3,4096]{2,1,0:T(4,128)(2,1)S(1)}, u32[]{:S(2)}, u32[]{:S(2)}) collective-permute-start(bf16[8,3,4096]{2,1,0:T(4,128)(2,1)S(1)} %copy-done.14), channel_id=1, source_target_pairs={{0,12},{1,13},{2,14},{3,15},{4,8},{5,9},{6,10},{7,11},{8,4},{9,5},... | collective-permute-start | bytes 589832 | tf_op jit(solution)/shard_map/ppermute | solution.py:231
  560.8 46.2 %collective-permute-start.12 = (bf16[8,3,4096]{2,1,0:T(4,128)(2,1)S(1)}, bf16[8,3,4096]{2,1,0:T(4,128)(2,1)S(1)}, u32[]{:S(2)}, u32[]{:S(2)}) collective-permute-start(bf16[8,3,4096]{2,1,0:T(4,128)(2,1)S(1)} %copy-done.13), channel_id=1, source_target_pairs={{0,13},{1,12},{2,15},{3,14},{4,9},{5,8},{6,11},{7,10},{8,5},{9,4},... | collective-permute-start | bytes 589832 | tf_op jit(solution)/shard_map/ppermute | solution.py:231
  572.1 40.1 %collective-permute-start.13 = (bf16[8,3,4096]{2,1,0:T(4,128)(2,1)S(1)}, bf16[8,3,4096]{2,1,0:T(4,128)(2,1)S(1)}, u32[]{:S(2)}, u32[]{:S(2)}) collective-permute-start(bf16[8,3,4096]{2,1,0:T(4,128)(2,1)S(1)} %copy-done.12), channel_id=1, source_target_pairs={{0,14},{1,15},{2,12},{3,13},{4,10},{5,11},{6,8},{7,9},{8,6},{9,7},... | collective-permute-start | bytes 589832 | tf_op jit(solution)/shard_map/ppermute | solution.py:231
  583.4 34.5 %collective-permute-start.14 = (bf16[8,3,4096]{2,1,0:T(4,128)(2,1)S(1)}, bf16[8,3,4096]{2,1,0:T(4,128)(2,1)S(1)}, u32[]{:S(2)}, u32[]{:S(2)}) collective-permute-start(bf16[8,3,4096]{2,1,0:T(4,128)(2,1)S(1)} %copy.179), channel_id=1, source_target_pairs={{0,15},{1,14},{2,13},{3,12},{4,11},{5,10},{6,9},{7,8},{8,7},{9,6},... | collective-permute-start | bytes 589832 | tf_op jit(solution)/shard_map/ppermute | solution.py:231
  748.0 3.9 copy-start.1
  (3 other events, 5.0 us)
